TPU v7x, 32 devices: a 4x4x1 block of a 4x4x8 slice. The times are simulated.
32 devices in a mesh: dp: 1 (over z), tp: 4 (over y), cp: 8 (over x, core).
Axes of the slice: x: 4, y: 4, z: 1, core: 2. Of those that a mesh axis runs over, the one named last changes fastest.
The devices are a block of a 4x4x8 slice.
Arguments:
- x: bfloat16 [2048, 6144], P(('dp', 'cp'))
- k_cache: bfloat16 [65536, 8, 128], P(('dp', 'cp'), 'tp')
- v_cache: bfloat16 [65536, 8, 128], P(('dp', 'cp'), 'tp')
- rope_table: float32 [2048, 64], P(('dp', 'cp'))
- norm_gain: bfloat16 [6144], replicated
- w_qkv: bfloat16 [6144, 8192], P(None, 'tp')
- b_qkv: bfloat16 [8192], P('tp')
- w_out: bfloat16 [6144, 6144], P('tp')
Outputs:
- output 1: bfloat16 [2048, 6144], P(('dp', 'cp'))
- output 2: bfloat16 [2048, 8, 128], P(('dp', 'cp'), 'tp')
- output 3: bfloat16 [2048, 8, 128], P(('dp', 'cp'), 'tp')
All inputs are finite; a program needn't handle non-finite values.
Results may differ from a plain program's by a relative error of at most 0.00313401.
Values are sent between devices in bfloat16 or wider.
A program may use at most 768 MiB of HBM per device.

v0:
```python
import functools
import math

import jax
import jax.numpy as jnp
from jax import lax
from jax.experimental import pallas as pl
from jax.experimental.pallas import tpu as pltpu
from jax.sharding import PartitionSpec as P


EPS = 1.5625e-07
MASK_VALUE = -1e30
LIMIT = 1e30
F32, BF16 = jnp.float32, jnp.bfloat16
STATS = 8
RELAYED = 0


def project_kernel(heads, dim, x_ref, gain_ref, w_ref, b_ref, cos_ref, sin_ref, nat_ref, tr_ref, h_ref):
    step = pl.program_id(0)
    rows = x_ref.shape[0]
    width = w_ref.shape[1]

    @pl.when(step == 0)
    def _():
        def norm(i, _):
            at = pl.ds(pl.multiple_of(i * 16, 16), 16)
            xf = x_ref[at, :].astype(F32)
            inv = lax.rsqrt(jnp.mean(xf * xf, axis=-1, keepdims=True) + EPS)
            h_ref[at, :] = (xf * inv * gain_ref[...].astype(F32)).astype(BF16)
            return 0

        lax.fori_loop(0, rows // 16, norm, 0)

    a = jnp.dot(h_ref[...], w_ref[...], preferred_element_type=F32) + b_ref[...].astype(F32)
    lane = lax.broadcasted_iota(jnp.int32, (rows, dim), 1)
    for part in range(width // dim):
        v = a[:, part * dim:(part + 1) * dim]
        swapped = jnp.where(lane % 2 == 0, pltpu.roll(v, dim - 1, 1), pltpu.roll(v, 1, 1))
        turned = v * cos_ref[...] + swapped * sin_ref[...]
        head = lax.rem(step * (width // dim) + part, heads)
        keep = jnp.where(head == heads - 1, 0, dim // 2)
        out = jnp.where(lane < keep, turned, v)
        nat_ref[:, part * dim:(part + 1) * dim] = out.astype(BF16)
        tr_ref[part * dim:(part + 1) * dim, :] = out.T.astype(BF16)


def project(x, rope_table, norm_gain, w_qkv, b_qkv, heads, dim):
    rows, d_model = x.shape
    cols = w_qkv.shape[1]
    pairs = rope_table.shape[1] // 2
    lane = jnp.arange(dim)[None, :]
    pair = jnp.arange(pairs)[:, None]
    cos_pick = (lane // 2 == pair).astype(F32)
    sin_pick = cos_pick * jnp.where(lane % 2 == 0, -1.0, 1.0)
    zero = jnp.zeros_like(cos_pick)
    pick = jnp.concatenate([jnp.concatenate([cos_pick, zero], axis=1), jnp.concatenate([zero, sin_pick], axis=1)], axis=0)
    wide = jnp.dot(rope_table, pick, precision=lax.Precision.HIGHEST, preferred_element_type=F32)
    cos_w, sin_w = wide[:, :dim], wide[:, dim:]
    width = 2 * dim
    return pl.pallas_call(
        functools.partial(project_kernel, heads, dim),
        grid=(cols // width,),
        in_specs=[
            pl.BlockSpec((rows, d_model), lambda i: (0, 0)),
            pl.BlockSpec((1, d_model), lambda i: (0, 0)),
            pl.BlockSpec((d_model, width), lambda i: (0, i)),
            pl.BlockSpec((1, width), lambda i: (0, i)),
            pl.BlockSpec((rows, dim), lambda i: (0, 0)),
            pl.BlockSpec((rows, dim), lambda i: (0, 0)),
        ],
        out_specs=[pl.BlockSpec((rows, width), lambda i: (0, i)), pl.BlockSpec((width, rows), lambda i: (i, 0))],
        out_shape=[jax.ShapeDtypeStruct((rows, cols), BF16), jax.ShapeDtypeStruct((cols, rows), BF16)],
        scratch_shapes=[pltpu.VMEM((rows, d_model), BF16)],
        compiler_params=pltpu.CompilerParams(vmem_limit_bytes=40 * 2**20, dimension_semantics=("arbitrary",)),
        cost_estimate=pl.CostEstimate(flops=2 * rows * d_model * cols, bytes_accessed=2 * d_model * cols, transcendentals=0),
        name="project",
    )(x, norm_gain[None, :], w_qkv, b_qkv[None, :], cos_w, sin_w)


def attend_kernel(c, blocks, bk, sub, shift_ref, *refs):
    q_refs = refs[:blocks]
    k_ref, vt_ref, kn_ref, vnt_ref = refs[blocks:blocks + 4]
    out_refs = refs[blocks + 4:2 * blocks + 4]
    acc_ref = refs[2 * blocks + 4]
    heads, dim, toks = q_refs[0].shape[1:]
    cols = heads * toks
    nk, nn = k_ref.shape[1], kn_ref.shape[1]
    q = jnp.concatenate([r[0, h] for r in q_refs for h in range(heads)], axis=1)
    bq = q.shape[1]

    def scores(k):
        return jnp.dot(k, q, preferred_element_type=F32)

    def fold(p):
        return jnp.sum(p.reshape(p.shape[0] // 8, 8, bq), axis=0)

    top = jnp.max(scores(k_ref[0, :256, :]), axis=0, keepdims=True)
    high = top.astype(BF16).astype(F32)
    mid = (top - high).astype(BF16).astype(F32)
    low = top - high - mid
    row = lax.broadcasted_iota(jnp.int32, (dim, bq), 0)
    bias = jnp.where(row == 0, high, jnp.where(row == 1, mid, jnp.where(row == 2, low, 0.0)))
    q_ext = jnp.concatenate([q, (-bias).astype(BF16)], axis=0)

    def shifted(k):
        ones = jnp.ones((k.shape[0], dim), BF16)
        return jnp.dot(jnp.concatenate([k, ones], axis=1), q_ext, preferred_element_type=F32)

    def mask_new(s):
        ahead = lax.broadcasted_iota(jnp.int32, (nn, toks), 0) - lax.broadcasted_iota(jnp.int32, (nn, toks), 1)
        parts = []
        for b in range(blocks):
            vis = ahead <= shift_ref[b]
            for h in range(heads):
                at = b * cols + h * toks
                parts.append(jnp.where(vis, s[:, at:at + toks], MASK_VALUE))
        return jnp.concatenate(parts, axis=1)

    p = jnp.exp2(mask_new(shifted(kn_ref[0])) * c)
    row_sum = fold(p)
    acc_ref[...] = jnp.dot(vnt_ref[0], p.astype(BF16), preferred_element_type=F32)

    def body(i, row_sum):
        base = pl.multiple_of(i * bk, bk)
        acc = None
        for j in range(bk // sub):
            at = pl.ds(base + j * sub, sub)
            p = jnp.exp2(shifted(k_ref[0, at, :]) * c)
            row_sum = row_sum + fold(p)
            d = jnp.dot(vt_ref[0, :, at], p.astype(BF16), preferred_element_type=F32)
            acc = d if acc is None else acc + d
        acc_ref[...] += acc
        return row_sum

    row_sum = jnp.sum(lax.fori_loop(0, nk // bk, body, row_sum), axis=0, keepdims=True)

    def emit(top, row_sum):
        for b in range(blocks):
            at = slice(b * cols, (b + 1) * cols)
            out_refs[b][0, :dim] = acc_ref[:, at]
            out_refs[b][0, dim:dim + STATS] = jnp.concatenate([top[:, at], row_sum[:, at], jnp.zeros((STATS - 2, cols), F32)], axis=0)

    emit(top * c, row_sum)
    worst = jnp.maximum(jnp.max(jnp.abs(acc_ref[...])), jnp.max(row_sum))

    @pl.when(jnp.logical_not(worst < LIMIT))
    def _():
        acc_ref[...] = jnp.zeros_like(acc_ref)

        def update(s, vt, carry):
            m, l = carry
            new = jnp.maximum(m, jnp.max(s, axis=0, keepdims=True) * c)
            r = jnp.exp2(m - new)
            p = jnp.exp2(s * c - new)
            acc_ref[...] = acc_ref[...] * r + jnp.dot(vt, p.astype(BF16), preferred_element_type=F32)
            return new, l * r + jnp.sum(p, axis=0, keepdims=True)

        def slow(i, carry):
            at = pl.ds(pl.multiple_of(i * 256, 256), 256)
            return update(scores(k_ref[0, at, :]), vt_ref[0, :, at], carry)

        carry = (jnp.full((1, bq), MASK_VALUE, F32), jnp.zeros((1, bq), F32))
        carry = lax.fori_loop(0, nk // 256, slow, carry)
        emit(*update(mask_new(scores(kn_ref[0])), vnt_ref[0], carry))


def attend(qs, shifts, k, vt, kn, vnt, toks, at=0, bk=2048, sub=1024):
    blocks = len(qs)
    groups, heads, dim, _ = qs[0].shape
    nk, nn = k.shape[1], kn.shape[1]
    cols = heads * toks
    c = math.log2(math.e) * dim ** -0.5
    grid_spec = pltpu.PrefetchScalarGridSpec(
        num_scalar_prefetch=1,
        grid=(groups,),
        in_specs=[pl.BlockSpec((1, heads, dim, toks), lambda i, s: (i, 0, 0, at))] * blocks + [
            pl.BlockSpec((1, nk, dim), lambda i, s: (i, 0, 0)),
            pl.BlockSpec((1, dim, nk), lambda i, s: (i, 0, 0)),
            pl.BlockSpec((1, nn, dim), lambda i, s: (i, 0, 0)),
            pl.BlockSpec((1, dim, nn), lambda i, s: (i, 0, 0)),
        ],
        out_specs=[pl.BlockSpec((1, dim + STATS, cols), lambda i, s: (i, 0, 0))] * blocks,
        scratch_shapes=[pltpu.VMEM((dim, blocks * cols), F32)],
    )
    return pl.pallas_call(
        functools.partial(attend_kernel, c, blocks, bk, sub),
        grid_spec=grid_spec,
        out_shape=[jax.ShapeDtypeStruct((groups, dim + STATS, cols), F32)] * blocks,
        compiler_params=pltpu.CompilerParams(vmem_limit_bytes=62 * 2**20, dimension_semantics=("arbitrary",)),
        cost_estimate=pl.CostEstimate(flops=4 * groups * blocks * cols * (nk + nn) * dim, bytes_accessed=4 * groups * nk * dim, transcendentals=groups * blocks * cols * nk),
        name="attend",
    )(shifts, *qs, k, vt, kn, vnt)


def tail_kernel(remote, groups, heads, dim, *refs):
    parts = refs[:remote]
    x_ref, w_own = refs[remote:remote + 2]
    w_mine, w_other = refs[remote + 2:remote + 5], refs[remote + 5:remote + 8]
    y_ref, pbuf, wbuf, xbuf, o_own, o_left, o_right, o_far, acc, load, wload, send, recv = refs[remote + 8:]
    rows, quarter = acc.shape
    toks = rows // 2
    wide = heads * dim
    tp, cp = lax.axis_index('tp'), lax.axis_index('cp')
    odd = lax.rem(cp, 2)
    left, right = lax.rem(tp + 3, 4), lax.rem(tp + 1, 4)

    barrier = pltpu.get_barrier_semaphore()
    for to in (left, right):
        pl.semaphore_signal(barrier, inc=1, device_id={'tp': to}, device_id_type=pl.DeviceIdType.MESH)

    loads = []
    for g in range(groups):
        here = [pltpu.make_async_copy(p.at[g], pbuf.at[g, i], load.at[g, i]) for i, p in enumerate(parts)]
        for d in here:
            d.start()
        loads.append(here)
    wloads = [pltpu.make_async_copy(x_ref.at[:, pl.ds(pl.multiple_of(tp * quarter, quarter), quarter)], xbuf, wload.at[0])]
    for g in range(groups):
        wloads.append(pltpu.make_async_copy(w_own.at[pl.ds(g * wide, wide), pl.ds(pl.multiple_of(tp * quarter, quarter), quarter)], wbuf.at[0, g], wload.at[1 + g]))
    for k in range(3):
        wloads.append(pltpu.make_async_copy(w_mine[k], wbuf.at[k + 1, odd], wload.at[3 + 2 * k]))
        wloads.append(pltpu.make_async_copy(w_other[k], wbuf.at[k + 1, 1 - odd], wload.at[4 + 2 * k]))
    for d in wloads:
        d.start()

    def remote_copy(src, dst, i, to):
        return pltpu.make_async_remote_copy(src_ref=src, dst_ref=dst, send_sem=send.at[i], recv_sem=recv.at[i], device_id={'tp': to}, device_id_type=pl.DeviceIdType.MESH)

    def merge(g):
        for d in loads[g]:
            d.wait()

        for h in range(heads):
            at = slice(h * rows, (h + 1) * rows)
            tops = [pbuf[g, i, dim:dim + 1, at] for i in range(remote)]
            sums = [pbuf[g, i, dim + 1:dim + 2, at] for i in range(remote)]
            top = functools.reduce(jnp.maximum, tops)
            scales = [jnp.exp2(t - top) for t in tops]
            total = sum(l * s for l, s in zip(sums, scales))
            val = sum(pbuf[g, i, :dim, at] * scales[i] for i in range(remote))
            o_own[g, :, h * dim:(h + 1) * dim] = (val / total).T.astype(BF16)

    def product(o, g, k, row=0, n=None, first=False):
        n = rows if n is None else n

        @pl.loop(0, quarter // 512)
        def _(j):
            at = pl.ds(pl.multiple_of(j * 512, 512), 512)
            d = jnp.dot(o[g, row:row + n, :], wbuf[k, g, :, at], preferred_element_type=F32)
            acc[row:row + n, at] = d if first else acc[row:row + n, at] + d

    merge(0)
    pl.semaphore_wait(barrier, 2)
    c0r = remote_copy(o_own.at[0], o_left.at[0], 0, right)
    c0l = remote_copy(o_own.at[0], o_right.at[0], 1, left)
    c0r.start()
    c0l.start()
    merge(1)
    c1l = remote_copy(o_own.at[1], o_right.at[1], 2, left)
    c1r = remote_copy(o_own.at[1], o_left.at[1], 3, right)
    c1l.start()
    c1r.start()
    for d in wloads:
        d.wait()
    product(o_own, 0, 0, first=True)
    product(o_own, 1, 0)
    c0r.wait_recv()
    f0 = remote_copy(o_left.at[0], o_far.at[0], 4, right)
    f0.start()
    c0l.wait_recv()
    product(o_left, 0, 1)
    product(o_right, 0, 3)
    c1l.wait_recv()
    f1 = remote_copy(o_right.at[1], o_far.at[1], 5, left)
    f1.start()
    c1r.wait_recv()
    product(o_right, 1, 3)
    product(o_left, 1, 1)
    f0.wait_recv()
    f1.wait_recv()

    def cols(t):
        return pl.ds(pl.multiple_of(t * quarter, quarter), quarter)

    def block(r, t):
        return y_ref.at[pl.ds(r * toks, toks), cols(t)]

    copies = [c0r, c0l, c1l, c1r, f0, f1]
    ycopies = []
    for r in range(2):
        product(o_far, 0, 2, r * toks, toks)
        product(o_far, 1, 2, r * toks, toks)
        at = slice(r * toks, (r + 1) * toks)
        y_ref[at, cols(tp)] = (xbuf[at].astype(F32) + acc[at]).astype(BF16)
        for i, to in enumerate((right, left) if r == 0 else (left, right)):
            d = remote_copy(block(r, tp), block(r, tp), 6 + 2 * r + i, to)
            d.start()
            ycopies.append(d)
    ar, al, bl, br = ycopies
    ar.wait_recv()
    fa = remote_copy(block(0, left), block(0, left), 10, right)
    fa.start()
    bl.wait_recv()
    fb = remote_copy(block(1, right), block(1, right), 11, left)
    fb.start()
    al.wait_recv()
    br.wait_recv()
    fa.wait_recv()
    fb.wait_recv()
    for d in copies + ycopies + [fa, fb]:
        d.wait_send()


def tail(parts, x, w_own, w_mine, w_other, heads, dim):
    groups = parts[0].shape[0]
    rows, d_model = x.shape
    quarter = w_mine[0].shape[1]
    wide = heads * dim
    remote = len(parts)
    any_spec = pl.BlockSpec(memory_space=pl.ANY)
    return pl.pallas_call(
        functools.partial(tail_kernel, remote, groups, heads, dim),
        out_shape=jax.ShapeDtypeStruct((rows, d_model), BF16),
        in_specs=[any_spec] * (remote + 8),
        out_specs=pl.BlockSpec(memory_space=pltpu.VMEM),
        scratch_shapes=[
            pltpu.VMEM((groups, remote) + parts[0].shape[1:], F32),
            pltpu.VMEM((4, groups, wide, quarter), BF16),
            pltpu.VMEM((rows, quarter), BF16),
            pltpu.VMEM((groups, rows, wide), BF16),
            pltpu.VMEM((groups, rows, wide), BF16),
            pltpu.VMEM((groups, rows, wide), BF16),
            pltpu.VMEM((groups, rows, wide), BF16),
            pltpu.VMEM((rows, quarter), F32),
            pltpu.SemaphoreType.DMA((groups, remote)),
            pltpu.SemaphoreType.DMA((9,)),
            pltpu.SemaphoreType.DMA((12,)),
            pltpu.SemaphoreType.DMA((12,)),
        ],
        compiler_params=pltpu.CompilerParams(vmem_limit_bytes=60 * 2**20, collective_id=0, has_side_effects=True),
        cost_estimate=pl.CostEstimate(flops=2 * rows * d_model * groups * wide, bytes_accessed=2 * d_model * quarter, transcendentals=0),
        name="tail",
    )(*parts, x, w_own, *w_mine, *w_other)


def ring(size, k):
    return [(i, (i + k) % size) for i in range(size)]


def make_step(cp_size, tp_size):
    def local_step(x, k_cache, v_cache, rope_table, norm_gain, w_qkv, b_qkv, w_out):
        groups, dim = k_cache.shape[1], k_cache.shape[2]
        rows, d_model = x.shape
        group_cols = w_qkv.shape[1] // groups
        heads = group_cols // dim
        q_heads = heads - 2
        me = lax.axis_index('cp')
        tp_me = lax.axis_index('tp')
        odd = lax.rem(me, 2)
        nat, tr = project(x, rope_table, norm_gain, w_qkv, b_qkv, heads, dim)
        nat = nat.reshape(rows, groups, heads, dim)
        tr = tr.reshape(groups, heads, dim, rows)
        k_new, v_new = nat[:, :, q_heads], nat[:, :, q_heads + 1]
        kn = k_new.transpose(1, 0, 2)
        vnt = tr[:, q_heads + 1]
        k_loc = k_cache.transpose(1, 0, 2)
        vt_loc = v_cache.transpose(1, 2, 0)

        q_own = tr[:, :q_heads]
        chips = cp_size // 2
        order = ((2, 1), (2, 0), (3, 0), (1, 0), (3, 1), (1, 1), (0, 1))

        def hop(val, j, flip):
            return lax.ppermute(val, 'cp', [(i, (i // 2 + j) % chips * 2 + (i % 2 ^ flip)) for i in range(cp_size)])

        def run(q, j, flip):
            owner = lax.rem(me // 2 + j, chips) * 2 + lax.rem(me + flip, 2)
            shifts = jnp.stack([(owner - me) * rows]).astype(jnp.int32)
            return attend([q], shifts, k_loc, vt_loc, kn, vnt, rows)[0]

        q10 = hop(q_own, -1, 0)
        q30 = hop(q_own, 1, 0)
        own = run(q_own, 0, 0)
        w_late, q10_late, own = lax.optimization_barrier((w_out, q10, own))
        q21 = hop(q10_late, -1, 1)
        q20 = hop(q21, 0, 1)
        queries = [q21, q20, q30, q10, hop(q30, 0, 1), hop(q10, 0, 1), hop(q_own, 0, 1)]

        w_rows = w_out.shape[0]
        half = w_rows // 2
        quarter = d_model // tp_size
        swap = [(i, i ^ 1) for i in range(cp_size)]
        mine, other = [], []
        for k in range(1, tp_size):
            to = lax.rem(tp_me + k, tp_size)
            piece = lax.dynamic_slice(w_late, (odd * half, to * quarter), (half, quarter))
            piece = lax.ppermute(piece, 'tp', ring(tp_size, k))
            mine.append(piece)

        parts, moving, last = [], None, own
        for n, q in enumerate(queries):
            if n == RELAYED + 2:
                q, last, moving = lax.optimization_barrier((q, last, moving))
                parts.append(hop(moving, -1, order[RELAYED][1]))
            elif n == len(order) - 1:
                q, last, mine = lax.optimization_barrier((q, last, mine))
                for piece in mine:
                    other.append(lax.ppermute(piece, 'cp', swap))
            else:
                q, last = lax.optimization_barrier((q, last))
            out = last = run(q, *order[n])
            if n == RELAYED:
                moving = hop(out, -1, 0)
            else:
                parts.append(hop(out, *order[n]))
        y = tail(parts + [own], x, w_out, mine, other, q_heads, dim)
        return y, k_new, v_new

    return local_step


def solution(mesh):
    row_spec = P(('dp', 'cp'), None)
    cache_spec = P(('dp', 'cp'), 'tp', None)
    inner = make_step(mesh.shape['cp'], mesh.shape['tp'])

    return jax.shard_map(inner, mesh=mesh, in_specs=(row_spec, cache_spec, cache_spec, row_spec, P(None), P(None, 'tp'), P('tp'), P('tp', None)), out_specs=(row_spec, cache_spec, cache_spec), check_vma=False)
```

profile of v0, /device:TPU:97, one launch (start us, length us, event | category | flops | bytes accessed | tf_op | source)
XLA Modules:
  0.0 478.2 jit_solution(18299284662213295084)
XLA Ops:
  3.4 1.9 copy-done.2
  5.2 17.2 %project.1 = (bf16[256,2048]{1,0:T(8,128)(2,1)S(1)}, bf16[2048,256]{1,0:T(8,128)(2,1)S(1)}) custom-call(bf16[256,6144]{1,0:T(8,128)(2,1)S(1)} %copy-done.2, bf16[1,6144]{1,0:T(2,128)(2,1)S(1)} %broadcast_in_dim.17.gain_ref, bf16[6144,2048]{1,0:T(8,128)(2,1)} %w_ref.1, bf16[1,2048]{1,0:T(2,128)(2,1)S(1)} %broadcast_in_dim.18.b_ref, ...), custom_call_target="tpu_custom_call" | custom-call | flops 6442450944 | bytes 25165824 | tf_op jit(solution)/shard_map/project/pallas_call | solution.py:62
  22.5 0.9 slice.26.refs_0_
  23.4 3.7 collective-permute-start
  29.1 4.7 copy.37
  33.8 11.2 %copy.26 = bf16[8192,2,128]{0,2,1:T(8,128)(2,1)} copy(bf16[8192,2,128]{2,1,0:T(2,128)(2,1)} %param.10) | data formatting | bytes 8388608 | tf_op args[2]
  45.0 26.4 %attend.8.refs_7_ = f32[2,136,1536]{2,1,0:T(8,128)} custom-call(s32[1]{0:T(128)} %bitcast.3.shift_ref, bf16[2,6,128,256]{3,2,1,0:T(8,128)(2,1)} %slice.26.refs_0_, bf16[2,8192,128]{2,1,0:T(8,128)(2,1)} %bitcast.30, bf16[2,128,8192]{2,1,0:T(8,128)(2,1)} %bitcast.38, bf16[2,256,128]{2,1,0:T(8,128)(2,1)} %bitcast.47, ...), custom_call_target="tpu_custom_call" | custom-call | flops 13287555072 | bytes 8388608 | tf_op jit(solution)/shard_map/attend/pallas_call | solution.py:187
  71.4 1.3 collective-permute-start.1
  72.7 1.2 collective-permute-start.4
  73.9 17.7 %collective-permute-done.1.refs_0_ = bf16[2,6,128,256]{3,2,1,0:T(8,128)(2,1)S(1)} collective-permute-done((bf16[2,6,128,256]{3,2,1,0:T(8,128)(2,1)S(1)}, bf16[2,6,128,256]{3,2,1,0:T(8,128)(2,1)S(1)}, u32[]{:S(2)}, u32[]{:S(2)}) %collective-permute-start.1) | collective-permute-done | bytes 786464 | tf_op jit(solution)/shard_map/ppermute | solution.py:376
  92.4 26.3 %attend.9 = f32[2,136,1536]{2,1,0:T(8,128)} custom-call(s32[1]{0:T(128)} %bitcast.10.shift_ref, bf16[2,6,128,256]{3,2,1,0:T(8,128)(2,1)} %copy-done.6, bf16[2,8192,128]{2,1,0:T(8,128)(2,1)} %bitcast.31, bf16[2,128,8192]{2,1,0:T(8,128)(2,1)} %bitcast.39, bf16[2,256,128]{2,1,0:T(8,128)(2,1)} %bitcast.48, bf16[2,128,256]{2,1,0:T(8,128)(2,1)} %slice_bitcast_fusion.1.refs_4_), custom_call_target="tpu_custom_call" | custom-call | flops 13287555072 | bytes 8388608 | tf_op jit(solution)/shard_map/attend/pallas_call | solution.py:187
  118.8 1.7 collective-permute-start.5
  120.4 6.2 %fusion.7 = (bf16[768,1536]{1,0:T(8,128)(2,1)}, bf16[768,1536]{1,0:T(8,128)(2,1)}, bf16[768,1536]{1,0:T(8,128)(2,1)}) fusion(bf16[1536,6144]{1,0:T(8,128)(2,1)} %refs_9_.1, s32[]{:T(128)S(6)} %select_n.62, s32[]{:T(128)S(6)} %select_n.65, s32[]{:T(128)S(6)} %select_n.64, s32[]{:T(128)S(6)} %select_n.63), kind=kLoop, calls=%fused_computation.23 | loop fusion | bytes 14155792 | tf_op jit(solution)/shard_map/dynamic_slice | solution.py:398
  126.6 1.9 collective-permute-start.14
  128.5 3.7 collective-permute-start.15
  132.2 26.3 %attend.10 = f32[2,136,1536]{2,1,0:T(8,128)} custom-call(s32[1]{0:T(128)} %bitcast.shift_ref, bf16[2,6,128,256]{3,2,1,0:T(8,128)(2,1)} %collective-permute-done.2.refs_0_, bf16[2,8192,128]{2,1,0:T(8,128)(2,1)} %bitcast.32, bf16[2,128,8192]{2,1,0:T(8,128)(2,1)} %bitcast.40, bf16[2,256,128]{2,1,0:T(8,128)(2,1)} %bitcast.49, ...), custom_call_target="tpu_custom_call" | custom-call | flops 13287555072 | bytes 8388608 | tf_op jit(solution)/shard_map/attend/pallas_call | solution.py:187
  159.3 1.6 collective-permute-start.9
  160.9 26.4 %attend.11 = f32[2,136,1536]{2,1,0:T(8,128)} custom-call(s32[1]{0:T(128)} %bitcast.12.shift_ref, bf16[2,6,128,256]{3,2,1,0:T(8,128)(2,1)} %collective-permute-done.4.refs_0_, bf16[2,8192,128]{2,1,0:T(8,128)(2,1)} %bitcast.33, bf16[2,128,8192]{2,1,0:T(8,128)(2,1)} %bitcast.41, bf16[2,256,128]{2,1,0:T(8,128)(2,1)} %bitcast.50, ...), custom_call_target="tpu_custom_call" | custom-call | flops 13287555072 | bytes 8388608 | tf_op jit(solution)/shard_map/attend/pallas_call | solution.py:187
  187.3 26.4 %attend.12 = f32[2,136,1536]{2,1,0:T(8,128)} custom-call(s32[1]{0:T(128)} %bitcast.13.shift_ref, bf16[2,6,128,256]{3,2,1,0:T(8,128)(2,1)} %copy-done.4, bf16[2,8192,128]{2,1,0:T(8,128)(2,1)} %bitcast.34, bf16[2,128,8192]{2,1,0:T(8,128)(2,1)} %bitcast.42, bf16[2,256,128]{2,1,0:T(8,128)(2,1)} %bitcast.51, bf16[2,128,256]{2,1,0:T(8,128)(2,1)} %slice_bitcast_fusion.1.refs_4_), custom_call_target="tpu_custom_call" | custom-call | flops 13287555072 | bytes 8388608 | tf_op jit(solution)/shard_map/attend/pallas_call | solution.py:187
  214.6 26.8 %attend.13 = f32[2,136,1536]{2,1,0:T(8,128)} custom-call(s32[1]{0:T(128)} %bitcast.14.shift_ref, bf16[2,6,128,256]{3,2,1,0:T(8,128)(2,1)} %copy-done.7, bf16[2,8192,128]{2,1,0:T(8,128)(2,1)} %bitcast.35, bf16[2,128,8192]{2,1,0:T(8,128)(2,1)} %bitcast.43, bf16[2,256,128]{2,1,0:T(8,128)(2,1)} %bitcast.52, bf16[2,128,256]{2,1,0:T(8,128)(2,1)} %slice_bitcast_fusion.1.refs_4_), custom_call_target="tpu_custom_call" | custom-call | flops 13287555072 | bytes 8388608 | tf_op jit(solution)/shard_map/attend/pallas_call | solution.py:187
  241.3 26.4 %attend.14 = f32[2,136,1536]{2,1,0:T(8,128)} custom-call(s32[1]{0:T(128)} %bitcast.15.shift_ref, bf16[2,6,128,256]{3,2,1,0:T(8,128)(2,1)} %collective-permute-done.11.refs_0_, bf16[2,8192,128]{2,1,0:T(8,128)(2,1)} %bitcast.36, bf16[2,128,8192]{2,1,0:T(8,128)(2,1)} %bitcast.44, bf16[2,256,128]{2,1,0:T(8,128)(2,1)} %bitcast.53, ...), custom_call_target="tpu_custom_call" | custom-call | flops 13287555072 | bytes 8388608 | tf_op jit(solution)/shard_map/attend/pallas_call | solution.py:187
  267.8 26.5 %attend.15 = f32[2,136,1536]{2,1,0:T(8,128)} custom-call(s32[1]{0:T(128)} %bitcast.16.shift_ref, bf16[2,6,128,256]{3,2,1,0:T(8,128)(2,1)} %collective-permute-done.13.refs_0_, bf16[2,8192,128]{2,1,0:T(8,128)(2,1)} %bitcast.37, bf16[2,128,8192]{2,1,0:T(8,128)(2,1)} %bitcast.45, bf16[2,256,128]{2,1,0:T(8,128)(2,1)} %bitcast.54, ...), custom_call_target="tpu_custom_call" | custom-call | flops 13287555072 | bytes 8388608 | tf_op jit(solution)/shard_map/attend/pallas_call | solution.py:187
  294.3 0.9 collective-permute-start.12
  295.2 2.1 collective-permute-start.10
  298.3 36.3 %collective-permute-done.12.refs_5_ = f32[2,136,1536]{2,1,0:T(8,128)} collective-permute-done((f32[2,136,1536]{2,1,0:T(8,128)}, f32[2,136,1536]{2,1,0:T(8,128)}, u32[]{:S(2)}, u32[]{:S(2)}) %collective-permute-start.12) | collective-permute-done | bytes 1671200 | tf_op jit(solution)/shard_map/ppermute | solution.py:376
  334.9 2.1 collective-permute-start.7
  337.0 33.3 %collective-permute-done.8.refs_3_ = f32[2,136,1536]{2,1,0:T(8,128)} collective-permute-done((f32[2,136,1536]{2,1,0:T(8,128)}, f32[2,136,1536]{2,1,0:T(8,128)}, u32[]{:S(2)}, u32[]{:S(2)}) %collective-permute-start.8) | collective-permute-done | bytes 1671200 | tf_op jit(solution)/shard_map/ppermute | solution.py:376
  370.3 1.4 collective-permute-start.6
  373.2 36.3 %collective-permute-done.6.refs_1_ = f32[2,136,1536]{2,1,0:T(8,128)} collective-permute-done((f32[2,136,1536]{2,1,0:T(8,128)}, f32[2,136,1536]{2,1,0:T(8,128)}, u32[]{:S(2)}, u32[]{:S(2)}) %collective-permute-start.6) | collective-permute-done | bytes 1671200 | tf_op jit(solution)/shard_map/ppermute | solution.py:376
  409.6 1.4 copy-done.3
  411.0 63.2 %tail.1 = bf16[256,6144]{1,0:T(8,128)(2,1)} custom-call(f32[2,136,1536]{2,1,0:T(8,128)} %collective-permute-done.3.refs_0_, f32[2,136,1536]{2,1,0:T(8,128)} %collective-permute-done.6.refs_1_, f32[2,136,1536]{2,1,0:T(8,128)} %collective-permute-done.7.refs_2_, f32[2,136,1536]{2,1,0:T(8,128)} %collective-permute-done.8.refs_3_, ...), custom_call_target="tpu_custom_call" | custom-call | flops 4831838208 | bytes 18874368 | tf_op jit(solution)/shard_map/tail/pallas_call | solution.py:323
  474.1 3.9 copy.39
  (56 shorter events, 10.1 us)
Async XLA Ops:
  0.6 0.8 copy-start
  3.4 1.9 copy-start.2
  23.4 48.0 %collective-permute-start = (bf16[2,6,128,256]{3,2,1,0:T(8,128)(2,1)}, bf16[2,6,128,256]{3,2,1,0:T(8,128)(2,1)S(1)}, u32[]{:S(2)}, u32[]{:S(2)}) collective-permute-start(bf16[2,6,128,256]{3,2,1,0:T(8,128)(2,1)} %slice.26.refs_0_), channel_id=1, source_target_pairs={{0,6},{1,7},{2,0},{3,1},{4,2},{5,3},{6,4},{7,5},{8,14},{9,15},{10,... | collective-permute-start | bytes 2359304 | tf_op jit(solution)/shard_map/ppermute | solution.py:376
  71.4 47.4 %copy-start.4 = (bf16[2,6,128,256]{3,2,1,0:T(8,128)(2,1)}, bf16[2,6,128,256]{3,2,1,0:T(8,128)(2,1)S(1)}, u32[]{:S(2)}) copy-start(bf16[2,6,128,256]{3,2,1,0:T(8,128)(2,1)S(1)} %collective-permute-done.refs_0_) | copy-start | bytes 2359300
  71.4 20.1 %collective-permute-start.1 = (bf16[2,6,128,256]{3,2,1,0:T(8,128)(2,1)S(1)}, bf16[2,6,128,256]{3,2,1,0:T(8,128)(2,1)S(1)}, u32[]{:S(2)}, u32[]{:S(2)}) collective-permute-start(bf16[2,6,128,256]{3,2,1,0:T(8,128)(2,1)S(1)} %collective-permute-done.refs_0_), channel_id=1, source_target_pairs={{0,7},{1,6},{2,1},{3,0},{4,3},{5,2},{6,5},{7,4},{8,15},{9,14},{10,... | collective-permute-start | bytes 2359304 | tf_op jit(solution)/shard_map/ppermute | solution.py:376
  72.7 85.8 %collective-permute-start.4 = (bf16[2,6,128,256]{3,2,1,0:T(8,128)(2,1)}, bf16[2,6,128,256]{3,2,1,0:T(8,128)(2,1)}, u32[]{:S(2)}, u32[]{:S(2)}) collective-permute-start(bf16[2,6,128,256]{3,2,1,0:T(8,128)(2,1)} %slice.26.refs_0_), channel_id=1, source_target_pairs={{0,2},{1,3},{2,4},{3,5},{4,6},{5,7},{6,0},{7,1},{8,10},{9,11},{10,... | collective-permute-start | bytes 2359304 | tf_op jit(solution)/shard_map/ppermute | solution.py:376
  73.9 193.8 %collective-permute-start.13 = (bf16[2,6,128,256]{3,2,1,0:T(8,128)(2,1)}, bf16[2,6,128,256]{3,2,1,0:T(8,128)(2,1)}, u32[]{:S(2)}, u32[]{:S(2)}) collective-permute-start(bf16[2,6,128,256]{3,2,1,0:T(8,128)(2,1)} %slice.26.refs_0_), channel_id=1, source_target_pairs={{0,1},{1,0},{2,3},{3,2},{4,5},{5,4},{6,7},{7,6},{8,9},{9,8},{10,11... | collective-permute-start | bytes 2359304 | tf_op jit(solution)/shard_map/ppermute | solution.py:376
  91.6 0.9 copy-start.6
  91.6 37.0 %collective-permute-start.2 = (bf16[2,6,128,256]{3,2,1,0:T(8,128)(2,1)S(1)}, bf16[2,6,128,256]{3,2,1,0:T(8,128)(2,1)}, u32[]{:S(2)}, u32[]{:S(2)}) collective-permute-start(bf16[2,6,128,256]{3,2,1,0:T(8,128)(2,1)S(1)} %collective-permute-done.1.refs_0_), channel_id=1, source_target_pairs={{0,1},{1,0},{2,3},{3,2},{4,5},{5,4},{6,7},{7,6},{8,9},{9,8},{10,11... | collective-permute-start | bytes 2359304 | tf_op jit(solution)/shard_map/ppermute | solution.py:376
  118.8 40.5 %collective-permute-start.5 = (f32[2,136,1536]{2,1,0:T(8,128)}, f32[2,136,1536]{2,1,0:T(8,128)}, u32[]{:S(2)}, u32[]{:S(2)}) collective-permute-start(f32[2,136,1536]{2,1,0:T(8,128)} %attend.9), channel_id=1, source_target_pairs={{0,6},{1,7},{2,0},{3,1},{4,2},{5,3},{6,4},{7,5},{8,14},{9,15},{10,... | collective-permute-start | bytes 5013512 | tf_op jit(solution)/shard_map/ppermute | solution.py:376
  126.6 141.1 %collective-permute-start.14 = (bf16[768,1536]{1,0:T(8,128)(2,1)}, bf16[768,1536]{1,0:T(8,128)(2,1)}, u32[]{:S(2)}, u32[]{:S(2)}) collective-permute-start(bf16[768,1536]{1,0:T(8,128)(2,1)} %get-tuple-element.43), channel_id=1, source_target_pairs={{0,8},{8,16},{16,24},{24,0},{1,9},{9,17},{17,25},{25,1},{2,10},{10... | collective-permute-start | bytes 7077896 | tf_op jit(solution)/shard_map/ppermute | solution.py:399
  128.5 139.2 %collective-permute-start.15 = (bf16[768,1536]{1,0:T(8,128)(2,1)}, bf16[768,1536]{1,0:T(8,128)(2,1)}, u32[]{:S(2)}, u32[]{:S(2)}) collective-permute-start(bf16[768,1536]{1,0:T(8,128)(2,1)} %get-tuple-element.42), channel_id=1, source_target_pairs={{0,16},{8,24},{16,0},{24,8},{1,17},{9,25},{17,1},{25,9},{2,18},{10... | collective-permute-start | bytes 7077896 | tf_op jit(solution)/shard_map/ppermute | solution.py:399
  158.5 109.2 %collective-permute-start.16 = (bf16[768,1536]{1,0:T(8,128)(2,1)}, bf16[768,1536]{1,0:T(8,128)(2,1)}, u32[]{:S(2)}, u32[]{:S(2)}) collective-permute-start(bf16[768,1536]{1,0:T(8,128)(2,1)} %get-tuple-element.41), channel_id=1, source_target_pairs={{0,24},{8,0},{16,8},{24,16},{1,25},{9,1},{17,9},{25,17},{2,26},{10... | collective-permute-start | bytes 7077896 | tf_op jit(solution)/shard_map/ppermute | solution.py:399
  159.3 54.4 %collective-permute-start.9 = (bf16[2,6,128,256]{3,2,1,0:T(8,128)(2,1)}, bf16[2,6,128,256]{3,2,1,0:T(8,128)(2,1)S(1)}, u32[]{:S(2)}, u32[]{:S(2)}) collective-permute-start(bf16[2,6,128,256]{3,2,1,0:T(8,128)(2,1)} %collective-permute-done.4.refs_0_), channel_id=1, source_target_pairs={{0,1},{1,0},{2,3},{3,2},{4,5},{5,4},{6,7},{7,6},{8,9},{9,8},{10,11... | collective-permute-start | bytes 2359304 | tf_op jit(solution)/shard_map/ppermute | solution.py:376
  187.3 26.4 %copy-start.5 = (bf16[2,6,128,256]{3,2,1,0:T(8,128)(2,1)S(1)}, bf16[2,6,128,256]{3,2,1,0:T(8,128)(2,1)}, u32[]{:S(2)}) copy-start(bf16[2,6,128,256]{3,2,1,0:T(8,128)(2,1)} %copy-done.4) | copy-start | bytes 2359300
  213.7 0.9 copy-start.7
  213.7 27.6 %collective-permute-start.11 = (bf16[2,6,128,256]{3,2,1,0:T(8,128)(2,1)S(1)}, bf16[2,6,128,256]{3,2,1,0:T(8,128)(2,1)}, u32[]{:S(2)}, u32[]{:S(2)}) collective-permute-start(bf16[2,6,128,256]{3,2,1,0:T(8,128)(2,1)S(1)} %copy-done.5), channel_id=1, source_target_pairs={{0,1},{1,0},{2,3},{3,2},{4,5},{5,4},{6,7},{7,6},{8,9},{9,8},{10,11... | collective-permute-start | bytes 2359304 | tf_op jit(solution)/shard_map/ppermute | solution.py:376
  241.3 55.9 %collective-permute-start.3 = (f32[2,136,1536]{2,1,0:T(8,128)}, f32[2,136,1536]{2,1,0:T(8,128)}, u32[]{:S(2)}, u32[]{:S(2)}) collective-permute-start(f32[2,136,1536]{2,1,0:T(8,128)} %attend.10), channel_id=1, source_target_pairs={{0,4},{1,5},{2,6},{3,7},{4,0},{5,1},{6,2},{7,3},{8,12},{9,13},{10,... | collective-permute-start | bytes 5013512 | tf_op jit(solution)/shard_map/ppermute | solution.py:376
  294.3 3.9 collective-permute-start.17
  294.3 40.3 %collective-permute-start.12 = (f32[2,136,1536]{2,1,0:T(8,128)}, f32[2,136,1536]{2,1,0:T(8,128)}, u32[]{:S(2)}, u32[]{:S(2)}) collective-permute-start(f32[2,136,1536]{2,1,0:T(8,128)} %attend.14), channel_id=1, source_target_pairs={{0,3},{1,2},{2,5},{3,4},{4,7},{5,6},{6,1},{7,0},{8,11},{9,10},{10,... | collective-permute-start | bytes 5013512 | tf_op jit(solution)/shard_map/ppermute | solution.py:376
  295.2 39.7 %collective-permute-start.10 = (f32[2,136,1536]{2,1,0:T(8,128)}, f32[2,136,1536]{2,1,0:T(8,128)}, u32[]{:S(2)}, u32[]{:S(2)}) collective-permute-start(f32[2,136,1536]{2,1,0:T(8,128)} %attend.13), channel_id=1, source_target_pairs={{0,7},{1,6},{2,1},{3,0},{4,3},{5,2},{6,5},{7,4},{8,15},{9,14},{10,... | collective-permute-start | bytes 5013512 | tf_op jit(solution)/shard_map/ppermute | solution.py:376
  297.2 73.1 %collective-permute-start.8 = (f32[2,136,1536]{2,1,0:T(8,128)}, f32[2,136,1536]{2,1,0:T(8,128)}, u32[]{:S(2)}, u32[]{:S(2)}) collective-permute-start(f32[2,136,1536]{2,1,0:T(8,128)} %attend.12), channel_id=1, source_target_pairs={{0,2},{1,3},{2,4},{3,5},{4,6},{5,7},{6,0},{7,1},{8,10},{9,11},{10,... | collective-permute-start | bytes 5013512 | tf_op jit(solution)/shard_map/ppermute | solution.py:376
  297.2 112.3 %collective-permute-start.18 = (bf16[768,1536]{1,0:T(8,128)(2,1)}, bf16[768,1536]{1,0:T(8,128)(2,1)S(1)}, u32[]{:S(2)}, u32[]{:S(2)}) collective-permute-start(bf16[768,1536]{1,0:T(8,128)(2,1)} %collective-permute-done.14.refs_10_), channel_id=1, source_target_pairs={{0,1},{1,0},{2,3},{3,2},{4,5},{5,4},{6,7},{7,6},{8,9},{9,8},{10,11... | collective-permute-start | bytes 7077896 | tf_op jit(solution)/shard_map/ppermute | solution.py:410
  298.1 111.4 %collective-permute-start.19 = (bf16[768,1536]{1,0:T(8,128)(2,1)}, bf16[768,1536]{1,0:T(8,128)(2,1)}, u32[]{:S(2)}, u32[]{:S(2)}) collective-permute-start(bf16[768,1536]{1,0:T(8,128)(2,1)} %collective-permute-done.15.refs_11_), channel_id=1, source_target_pairs={{0,1},{1,0},{2,3},{3,2},{4,5},{5,4},{6,7},{7,6},{8,9},{9,8},{10,11... | collective-permute-start | bytes 7077896 | tf_op jit(solution)/shard_map/ppermute | solution.py:410
  334.6 74.9 %collective-permute-start.20 = (bf16[768,1536]{1,0:T(8,128)(2,1)}, bf16[768,1536]{1,0:T(8,128)(2,1)}, u32[]{:S(2)}, u32[]{:S(2)}) collective-permute-start(bf16[768,1536]{1,0:T(8,128)(2,1)} %collective-permute-done.16.refs_12_), channel_id=1, source_target_pairs={{0,1},{1,0},{2,3},{3,2},{4,5},{5,4},{6,7},{7,6},{8,9},{9,8},{10,11... | collective-permute-start | bytes 7077896 | tf_op jit(solution)/shard_map/ppermute | solution.py:410
  334.9 38.3 %collective-permute-start.7 = (f32[2,136,1536]{2,1,0:T(8,128)}, f32[2,136,1536]{2,1,0:T(8,128)}, u32[]{:S(2)}, u32[]{:S(2)}) collective-permute-start(f32[2,136,1536]{2,1,0:T(8,128)} %attend.11), channel_id=1, source_target_pairs={{0,6},{1,7},{2,0},{3,1},{4,2},{5,3},{6,4},{7,5},{8,14},{9,15},{10,... | collective-permute-start | bytes 5013512 | tf_op jit(solution)/shard_map/ppermute | solution.py:376
  370.3 39.2 %collective-permute-start.6 = (f32[2,136,1536]{2,1,0:T(8,128)}, f32[2,136,1536]{2,1,0:T(8,128)}, u32[]{:S(2)}, u32[]{:S(2)}) collective-permute-start(f32[2,136,1536]{2,1,0:T(8,128)} %collective-permute-done.5), channel_id=1, source_target_pairs={{0,7},{1,6},{2,1},{3,0},{4,3},{5,2},{6,5},{7,4},{8,15},{9,14},{10,... | collective-permute-start | bytes 5013512 | tf_op jit(solution)/shard_map/ppermute | solution.py:376
  409.5 1.4 copy-start.3
  411.0 67.1 %copy-start.1 = (f32[256,64]{0,1:T(8,128)S(1)}, f32[256,64]{0,1:T(8,128)}, u32[]{:S(2)}) copy-start(f32[256,64]{0,1:T(8,128)} %param.11) | copy-start | bytes 196612
where the time goes:
time: 486 us; the launch traced here: 478 us
  Pallas kernels  292 us (60%)
  waiting for transfers between devices  124 us (26%)
  local copies, waits for them, and re-layouts  37.1 us (8%)
  starting transfers between devices  23.9 us (5%)
    pallas_call x8, Pallas kernels, attend(): pl.pallas_call(functools.partial(attend_kernel, c, blocks, bk, sub), grid...  211 us
    ppermute x15, waiting for transfers between devices, hop(): lax.ppermute(val, 'cp', [(i, (i // 2 + j) % chips * 2 + (i % 2 ^ flip)) f...  124 us
    pallas_call x1, Pallas kernels, tail(): pl.pallas_call(functools.partial(tail_kernel, remote, groups, heads, dim)...  63.2 us
    unnamed x22, local copies, waits for them, and re-layouts  27.3 us
    pallas_call x1, Pallas kernels, project(): pl.pallas_call(functools.partial(project_kernel, heads, dim), grid=(cols...  17.2 us
    ppermute x15, starting transfers between devices, hop(): lax.ppermute(val, 'cp', [(i, (i // 2 + j) % chips * 2 + (i % 2 ^ flip)) f...  16.6 us
  transfers between devices with their start and end apart: 21, of which 5 were waited for; matrix products, arithmetic and copies ran while one was open for 5% of the time, Pallas kernels for 44%

commit v1 on v0

--- a/solution.py
+++ b/solution.py
@@ -11,7 +11,8 @@
 
 EPS = 1.5625e-07
 MASK_VALUE = -1e30
-LIMIT = 1e30
+SUM_LIMIT = 1e12
+ACC_LIMIT = 1e36
 F32, BF16 = jnp.float32, jnp.bfloat16
 STATS = 8
 RELAYED = 0
@@ -143,27 +144,37 @@
             out_refs[b][0, dim:dim + STATS] = jnp.concatenate([top[:, at], row_sum[:, at], jnp.zeros((STATS - 2, cols), F32)], axis=0)
 
     emit(top * c, row_sum)
-    worst = jnp.maximum(jnp.max(jnp.abs(acc_ref[...])), jnp.max(row_sum))
-
-    @pl.when(jnp.logical_not(worst < LIMIT))
+    fits = jnp.logical_and(jnp.max(row_sum) < SUM_LIMIT, jnp.max(jnp.abs(acc_ref[...])) < ACC_LIMIT)
+
+    @pl.when(jnp.logical_not(fits))
     def _():
-        acc_ref[...] = jnp.zeros_like(acc_ref)
-
-        def update(s, vt, carry):
-            m, l = carry
-            new = jnp.maximum(m, jnp.max(s, axis=0, keepdims=True) * c)
-            r = jnp.exp2(m - new)
-            p = jnp.exp2(s * c - new)
-            acc_ref[...] = acc_ref[...] * r + jnp.dot(vt, p.astype(BF16), preferred_element_type=F32)
-            return new, l * r + jnp.sum(p, axis=0, keepdims=True)
-
-        def slow(i, carry):
-            at = pl.ds(pl.multiple_of(i * 256, 256), 256)
-            return update(scores(k_ref[0, at, :]), vt_ref[0, :, at], carry)
-
-        carry = (jnp.full((1, bq), MASK_VALUE, F32), jnp.zeros((1, bq), F32))
-        carry = lax.fori_loop(0, nk // 256, slow, carry)
-        emit(*update(mask_new(scores(kn_ref[0])), vnt_ref[0], carry))
+        def head(h, _):
+            at = pl.ds(pl.multiple_of(h * toks, toks), toks)
+            for b in range(blocks):
+                qh = q_refs[b][0, h]
+
+                def update(s, vt, carry):
+                    m, l, acc = carry
+                    new = jnp.maximum(m, jnp.max(s, axis=0, keepdims=True) * c)
+                    r = jnp.exp2(m - new)
+                    p = jnp.exp2(s * c - new)
+                    acc = acc * r + jnp.dot(vt, p.astype(BF16), preferred_element_type=F32)
+                    return new, l * r + jnp.sum(p, axis=0, keepdims=True), acc
+
+                def slow(i, carry):
+                    keys = pl.ds(pl.multiple_of(i * 256, 256), 256)
+                    return update(jnp.dot(k_ref[0, keys, :], qh, preferred_element_type=F32), vt_ref[0, :, keys], carry)
+
+                carry = (jnp.full((1, toks), MASK_VALUE, F32), jnp.zeros((1, toks), F32), jnp.zeros((dim, toks), F32))
+                carry = lax.fori_loop(0, nk // 256, slow, carry)
+                ahead = lax.broadcasted_iota(jnp.int32, (nn, toks), 0) - lax.broadcasted_iota(jnp.int32, (nn, toks), 1)
+                s = jnp.where(ahead <= shift_ref[b], jnp.dot(kn_ref[0], qh, preferred_element_type=F32), MASK_VALUE)
+                m, l, acc = update(s, vnt_ref[0], carry)
+                out_refs[b][0, :dim, at] = acc
+                out_refs[b][0, dim:dim + STATS, at] = jnp.concatenate([m, l, jnp.zeros((STATS - 2, toks), F32)], axis=0)
+            return 0
+
+        lax.fori_loop(0, heads, head, 0)
 
 
 def attend(qs, shifts, k, vt, kn, vnt, toks, at=0, bk=2048, sub=1024):

time: 486 us -> 498 us (1.025)
  the two profiles are of different devices: /device:TPU:97 before, /device:TPU:102 now
where the time goes in v1:
time: 498 us; the launch traced here: 488 us
  Pallas kernels  292 us (59%)
  waiting for transfers between devices  126 us (25%)
  local copies, waits for them, and re-layouts  37.1 us (7%)
  starting transfers between devices  31.8 us (6%)
    pallas_call x8, Pallas kernels, attend(): pl.pallas_call(functools.partial(attend_kernel, c, blocks, bk, sub), grid...  211 us
    ppermute x15, waiting for transfers between devices, hop(): lax.ppermute(val, 'cp', [(i, (i // 2 + j) % chips * 2 + (i % 2 ^ flip)) f...  126 us
    pallas_call x1, Pallas kernels, tail(): pl.pallas_call(functools.partial(tail_kernel, remote, groups, heads, dim)...  64.1 us
    unnamed x22, local copies, waits for them, and re-layouts  27.3 us
    ppermute x3, starting transfers between devices, local_step(): piece = lax.ppermute(piece, 'tp', ring(tp_size, k))  17.7 us
    pallas_call x1, Pallas kernels, project(): pl.pallas_call(functools.partial(project_kernel, heads, dim), grid=(cols...  17.2 us
    ppermute x15, starting transfers between devices, hop(): lax.ppermute(val, 'cp', [(i, (i // 2 + j) % chips * 2 + (i % 2 ^ flip)) f...  12.4 us
  transfers between devices with their start and end apart: 21, of which 6 were waited for; matrix products, arithmetic and copies ran while one was open for 5% of the time, Pallas kernels for 43%

profile of v1, /device:TPU:102, one launch (start us, length us, event | category | flops | bytes accessed | tf_op | source)
XLA Modules:
  0.0 488.5 jit_solution(1996484272060174590)
XLA Ops:
  3.4 1.9 copy-done.2
  5.2 17.2 %project.1 = (bf16[256,2048]{1,0:T(8,128)(2,1)S(1)}, bf16[2048,256]{1,0:T(8,128)(2,1)S(1)}) custom-call(bf16[256,6144]{1,0:T(8,128)(2,1)S(1)} %copy-done.2, bf16[1,6144]{1,0:T(2,128)(2,1)S(1)} %broadcast_in_dim.17.gain_ref, bf16[6144,2048]{1,0:T(8,128)(2,1)} %w_ref.1, bf16[1,2048]{1,0:T(2,128)(2,1)S(1)} %broadcast_in_dim.18.b_ref, ...), custom_call_target="tpu_custom_call" | custom-call | flops 6442450944 | bytes 25165824 | tf_op jit(solution)/shard_map/project/pallas_call | solution.py:63
  22.5 0.9 slice.26.refs_0_
  26.1 4.7 copy.37
  30.8 11.2 %copy.26 = bf16[8192,2,128]{0,2,1:T(8,128)(2,1)} copy(bf16[8192,2,128]{2,1,0:T(2,128)(2,1)} %param.10) | data formatting | bytes 8388608 | tf_op args[2]
  42.0 26.4 %attend.8.refs_7_ = f32[2,136,1536]{2,1,0:T(8,128)} custom-call(s32[1]{0:T(128)} %bitcast.3.shift_ref, bf16[2,6,128,256]{3,2,1,0:T(8,128)(2,1)} %slice.26.refs_0_, bf16[2,8192,128]{2,1,0:T(8,128)(2,1)} %bitcast.30, bf16[2,128,8192]{2,1,0:T(8,128)(2,1)} %bitcast.38, bf16[2,256,128]{2,1,0:T(8,128)(2,1)} %bitcast.47, ...), custom_call_target="tpu_custom_call" | custom-call | flops 13287555072 | bytes 8388608 | tf_op jit(solution)/shard_map/attend/pallas_call | solution.py:198
  68.5 2.6 collective-permute-start.4
  71.6 17.9 %collective-permute-done.1.refs_0_ = bf16[2,6,128,256]{3,2,1,0:T(8,128)(2,1)S(1)} collective-permute-done((bf16[2,6,128,256]{3,2,1,0:T(8,128)(2,1)S(1)}, bf16[2,6,128,256]{3,2,1,0:T(8,128)(2,1)S(1)}, u32[]{:S(2)}, u32[]{:S(2)}) %collective-permute-start.1) | collective-permute-done | bytes 786464 | tf_op jit(solution)/shard_map/ppermute | solution.py:387
  89.5 0.8 copy-done.6
  90.3 26.4 %attend.9 = f32[2,136,1536]{2,1,0:T(8,128)} custom-call(s32[1]{0:T(128)} %bitcast.10.shift_ref, bf16[2,6,128,256]{3,2,1,0:T(8,128)(2,1)} %copy-done.6, bf16[2,8192,128]{2,1,0:T(8,128)(2,1)} %bitcast.31, bf16[2,128,8192]{2,1,0:T(8,128)(2,1)} %bitcast.39, bf16[2,256,128]{2,1,0:T(8,128)(2,1)} %bitcast.48, bf16[2,128,256]{2,1,0:T(8,128)(2,1)} %slice_bitcast_fusion.1.refs_4_), custom_call_target="tpu_custom_call" | custom-call | flops 13287555072 | bytes 8388608 | tf_op jit(solution)/shard_map/attend/pallas_call | solution.py:198
  116.7 6.2 %fusion.7 = (bf16[768,1536]{1,0:T(8,128)(2,1)}, bf16[768,1536]{1,0:T(8,128)(2,1)}, bf16[768,1536]{1,0:T(8,128)(2,1)}) fusion(bf16[1536,6144]{1,0:T(8,128)(2,1)} %refs_9_.1, s32[]{:T(128)S(6)} %select_n.62, s32[]{:T(128)S(6)} %select_n.65, s32[]{:T(128)S(6)} %select_n.64, s32[]{:T(128)S(6)} %select_n.63), kind=kLoop, calls=%fused_computation.23 | loop fusion | bytes 14155792 | tf_op jit(solution)/shard_map/dynamic_slice | solution.py:409
  122.9 12.9 %collective-permute-start.14 = (bf16[768,1536]{1,0:T(8,128)(2,1)}, bf16[768,1536]{1,0:T(8,128)(2,1)}, u32[]{:S(2)}, u32[]{:S(2)}) collective-permute-start(bf16[768,1536]{1,0:T(8,128)(2,1)} %get-tuple-element.43), channel_id=1, source_target_pairs={{0,8},{8,16},{16,24},{24,0},{1,9},{9,17},{17,25},{25,1},{2,10},{10... | collective-permute-start | bytes 7077896 | tf_op jit(solution)/shard_map/ppermute | solution.py:410
  135.8 4.0 collective-permute-start.15
  139.8 26.3 %attend.10 = f32[2,136,1536]{2,1,0:T(8,128)} custom-call(s32[1]{0:T(128)} %bitcast.shift_ref, bf16[2,6,128,256]{3,2,1,0:T(8,128)(2,1)} %collective-permute-done.2.refs_0_, bf16[2,8192,128]{2,1,0:T(8,128)(2,1)} %bitcast.32, bf16[2,128,8192]{2,1,0:T(8,128)(2,1)} %bitcast.40, bf16[2,256,128]{2,1,0:T(8,128)(2,1)} %bitcast.49, ...), custom_call_target="tpu_custom_call" | custom-call | flops 13287555072 | bytes 8388608 | tf_op jit(solution)/shard_map/attend/pallas_call | solution.py:198
  166.2 0.8 collective-permute-start.16
  167.0 26.4 %attend.11 = f32[2,136,1536]{2,1,0:T(8,128)} custom-call(s32[1]{0:T(128)} %bitcast.12.shift_ref, bf16[2,6,128,256]{3,2,1,0:T(8,128)(2,1)} %collective-permute-done.4.refs_0_, bf16[2,8192,128]{2,1,0:T(8,128)(2,1)} %bitcast.33, bf16[2,128,8192]{2,1,0:T(8,128)(2,1)} %bitcast.41, bf16[2,256,128]{2,1,0:T(8,128)(2,1)} %bitcast.50, ...), custom_call_target="tpu_custom_call" | custom-call | flops 13287555072 | bytes 8388608 | tf_op jit(solution)/shard_map/attend/pallas_call | solution.py:198
  193.4 26.4 %attend.12 = f32[2,136,1536]{2,1,0:T(8,128)} custom-call(s32[1]{0:T(128)} %bitcast.13.shift_ref, bf16[2,6,128,256]{3,2,1,0:T(8,128)(2,1)} %copy-done.4, bf16[2,8192,128]{2,1,0:T(8,128)(2,1)} %bitcast.34, bf16[2,128,8192]{2,1,0:T(8,128)(2,1)} %bitcast.42, bf16[2,256,128]{2,1,0:T(8,128)(2,1)} %bitcast.51, bf16[2,128,256]{2,1,0:T(8,128)(2,1)} %slice_bitcast_fusion.1.refs_4_), custom_call_target="tpu_custom_call" | custom-call | flops 13287555072 | bytes 8388608 | tf_op jit(solution)/shard_map/attend/pallas_call | solution.py:198
  220.7 26.4 %attend.13 = f32[2,136,1536]{2,1,0:T(8,128)} custom-call(s32[1]{0:T(128)} %bitcast.14.shift_ref, bf16[2,6,128,256]{3,2,1,0:T(8,128)(2,1)} %copy-done.7, bf16[2,8192,128]{2,1,0:T(8,128)(2,1)} %bitcast.35, bf16[2,128,8192]{2,1,0:T(8,128)(2,1)} %bitcast.43, bf16[2,256,128]{2,1,0:T(8,128)(2,1)} %bitcast.52, bf16[2,128,256]{2,1,0:T(8,128)(2,1)} %slice_bitcast_fusion.1.refs_4_), custom_call_target="tpu_custom_call" | custom-call | flops 13287555072 | bytes 8388608 | tf_op jit(solution)/shard_map/attend/pallas_call | solution.py:198
  247.0 2.6 collective-permute-start.3
  249.7 26.4 %attend.14 = f32[2,136,1536]{2,1,0:T(8,128)} custom-call(s32[1]{0:T(128)} %bitcast.15.shift_ref, bf16[2,6,128,256]{3,2,1,0:T(8,128)(2,1)} %collective-permute-done.11.refs_0_, bf16[2,8192,128]{2,1,0:T(8,128)(2,1)} %bitcast.36, bf16[2,128,8192]{2,1,0:T(8,128)(2,1)} %bitcast.44, bf16[2,256,128]{2,1,0:T(8,128)(2,1)} %bitcast.53, ...), custom_call_target="tpu_custom_call" | custom-call | flops 13287555072 | bytes 8388608 | tf_op jit(solution)/shard_map/attend/pallas_call | solution.py:198
  276.1 26.3 %attend.15 = f32[2,136,1536]{2,1,0:T(8,128)} custom-call(s32[1]{0:T(128)} %bitcast.16.shift_ref, bf16[2,6,128,256]{3,2,1,0:T(8,128)(2,1)} %collective-permute-done.13.refs_0_, bf16[2,8192,128]{2,1,0:T(8,128)(2,1)} %bitcast.37, bf16[2,128,8192]{2,1,0:T(8,128)(2,1)} %bitcast.45, bf16[2,256,128]{2,1,0:T(8,128)(2,1)} %bitcast.54, ...), custom_call_target="tpu_custom_call" | custom-call | flops 13287555072 | bytes 8388608 | tf_op jit(solution)/shard_map/attend/pallas_call | solution.py:198
  303.3 1.0 collective-permute-start.10
  304.3 2.3 collective-permute-start.8
  307.1 34.1 %collective-permute-done.12.refs_5_ = f32[2,136,1536]{2,1,0:T(8,128)} collective-permute-done((f32[2,136,1536]{2,1,0:T(8,128)}, f32[2,136,1536]{2,1,0:T(8,128)}, u32[]{:S(2)}, u32[]{:S(2)}) %collective-permute-start.12) | collective-permute-done | bytes 1671200 | tf_op jit(solution)/shard_map/ppermute | solution.py:387
  341.2 1.1 collective-permute-start.20
  343.4 34.1 %collective-permute-done.8.refs_3_ = f32[2,136,1536]{2,1,0:T(8,128)} collective-permute-done((f32[2,136,1536]{2,1,0:T(8,128)}, f32[2,136,1536]{2,1,0:T(8,128)}, u32[]{:S(2)}, u32[]{:S(2)}) %collective-permute-start.8) | collective-permute-done | bytes 1671200 | tf_op jit(solution)/shard_map/ppermute | solution.py:387
  378.1 0.8 copy.30
  379.7 4.2 collective-permute-done.7.refs_2_
  383.8 34.8 %collective-permute-done.6.refs_1_ = f32[2,136,1536]{2,1,0:T(8,128)} collective-permute-done((f32[2,136,1536]{2,1,0:T(8,128)}, f32[2,136,1536]{2,1,0:T(8,128)}, u32[]{:S(2)}, u32[]{:S(2)}) %collective-permute-start.6) | collective-permute-done | bytes 1671200 | tf_op jit(solution)/shard_map/ppermute | solution.py:387
  418.7 1.4 copy-done.3
  420.1 64.1 %tail.1 = bf16[256,6144]{1,0:T(8,128)(2,1)} custom-call(f32[2,136,1536]{2,1,0:T(8,128)} %collective-permute-done.3.refs_0_, f32[2,136,1536]{2,1,0:T(8,128)} %collective-permute-done.6.refs_1_, f32[2,136,1536]{2,1,0:T(8,128)} %collective-permute-done.7.refs_2_, f32[2,136,1536]{2,1,0:T(8,128)} %collective-permute-done.8.refs_3_, ...), custom_call_target="tpu_custom_call" | custom-call | flops 4831838208 | bytes 18874368 | tf_op jit(solution)/shard_map/tail/pallas_call | solution.py:334
  484.2 3.9 copy.39
  (56 shorter events, 10.7 us)
Async XLA Ops:
  0.6 0.8 copy-start
  3.4 1.9 copy-start.2
  23.4 45.0 %collective-permute-start = (bf16[2,6,128,256]{3,2,1,0:T(8,128)(2,1)}, bf16[2,6,128,256]{3,2,1,0:T(8,128)(2,1)S(1)}, u32[]{:S(2)}, u32[]{:S(2)}) collective-permute-start(bf16[2,6,128,256]{3,2,1,0:T(8,128)(2,1)} %slice.26.refs_0_), channel_id=1, source_target_pairs={{0,6},{1,7},{2,0},{3,1},{4,2},{5,3},{6,4},{7,5},{8,14},{9,15},{10,... | collective-permute-start | bytes 2359304 | tf_op jit(solution)/shard_map/ppermute | solution.py:387
  68.4 48.3 %copy-start.4 = (bf16[2,6,128,256]{3,2,1,0:T(8,128)(2,1)}, bf16[2,6,128,256]{3,2,1,0:T(8,128)(2,1)S(1)}, u32[]{:S(2)}) copy-start(bf16[2,6,128,256]{3,2,1,0:T(8,128)(2,1)S(1)} %collective-permute-done.refs_0_) | copy-start | bytes 2359300
  68.4 21.1 %collective-permute-start.1 = (bf16[2,6,128,256]{3,2,1,0:T(8,128)(2,1)S(1)}, bf16[2,6,128,256]{3,2,1,0:T(8,128)(2,1)S(1)}, u32[]{:S(2)}, u32[]{:S(2)}) collective-permute-start(bf16[2,6,128,256]{3,2,1,0:T(8,128)(2,1)S(1)} %collective-permute-done.refs_0_), channel_id=1, source_target_pairs={{0,7},{1,6},{2,1},{3,0},{4,3},{5,2},{6,5},{7,4},{8,15},{9,14},{10,... | collective-permute-start | bytes 2359304 | tf_op jit(solution)/shard_map/ppermute | solution.py:387
  68.5 97.6 %collective-permute-start.4 = (bf16[2,6,128,256]{3,2,1,0:T(8,128)(2,1)}, bf16[2,6,128,256]{3,2,1,0:T(8,128)(2,1)}, u32[]{:S(2)}, u32[]{:S(2)}) collective-permute-start(bf16[2,6,128,256]{3,2,1,0:T(8,128)(2,1)} %slice.26.refs_0_), channel_id=1, source_target_pairs={{0,2},{1,3},{2,4},{3,5},{4,6},{5,7},{6,0},{7,1},{8,10},{9,11},{10,... | collective-permute-start | bytes 2359304 | tf_op jit(solution)/shard_map/ppermute | solution.py:387
  71.2 204.9 %collective-permute-start.13 = (bf16[2,6,128,256]{3,2,1,0:T(8,128)(2,1)}, bf16[2,6,128,256]{3,2,1,0:T(8,128)(2,1)}, u32[]{:S(2)}, u32[]{:S(2)}) collective-permute-start(bf16[2,6,128,256]{3,2,1,0:T(8,128)(2,1)} %slice.26.refs_0_), channel_id=1, source_target_pairs={{0,1},{1,0},{2,3},{3,2},{4,5},{5,4},{6,7},{7,6},{8,9},{9,8},{10,11... | collective-permute-start | bytes 2359304 | tf_op jit(solution)/shard_map/ppermute | solution.py:387
  89.5 0.9 copy-start.6
  89.5 46.4 %collective-permute-start.2 = (bf16[2,6,128,256]{3,2,1,0:T(8,128)(2,1)S(1)}, bf16[2,6,128,256]{3,2,1,0:T(8,128)(2,1)}, u32[]{:S(2)}, u32[]{:S(2)}) collective-permute-start(bf16[2,6,128,256]{3,2,1,0:T(8,128)(2,1)S(1)} %collective-permute-done.1.refs_0_), channel_id=1, source_target_pairs={{0,1},{1,0},{2,3},{3,2},{4,5},{5,4},{6,7},{7,6},{8,9},{9,8},{10,11... | collective-permute-start | bytes 2359304 | tf_op jit(solution)/shard_map/ppermute | solution.py:387
  116.7 50.3 %collective-permute-start.5 = (f32[2,136,1536]{2,1,0:T(8,128)}, f32[2,136,1536]{2,1,0:T(8,128)}, u32[]{:S(2)}, u32[]{:S(2)}) collective-permute-start(f32[2,136,1536]{2,1,0:T(8,128)} %attend.9), channel_id=1, source_target_pairs={{0,6},{1,7},{2,0},{3,1},{4,2},{5,3},{6,4},{7,5},{8,14},{9,15},{10,... | collective-permute-start | bytes 5013512 | tf_op jit(solution)/shard_map/ppermute | solution.py:387
  122.9 153.1 %collective-permute-start.14 = (bf16[768,1536]{1,0:T(8,128)(2,1)}, bf16[768,1536]{1,0:T(8,128)(2,1)}, u32[]{:S(2)}, u32[]{:S(2)}) collective-permute-start(bf16[768,1536]{1,0:T(8,128)(2,1)} %get-tuple-element.43), channel_id=1, source_target_pairs={{0,8},{8,16},{16,24},{24,0},{1,9},{9,17},{17,25},{25,1},{2,10},{10... | collective-permute-start | bytes 7077896 | tf_op jit(solution)/shard_map/ppermute | solution.py:410
  135.8 140.2 %collective-permute-start.15 = (bf16[768,1536]{1,0:T(8,128)(2,1)}, bf16[768,1536]{1,0:T(8,128)(2,1)}, u32[]{:S(2)}, u32[]{:S(2)}) collective-permute-start(bf16[768,1536]{1,0:T(8,128)(2,1)} %get-tuple-element.42), channel_id=1, source_target_pairs={{0,16},{8,24},{16,0},{24,8},{1,17},{9,25},{17,1},{25,9},{2,18},{10... | collective-permute-start | bytes 7077896 | tf_op jit(solution)/shard_map/ppermute | solution.py:410
  166.2 109.9 %collective-permute-start.16 = (bf16[768,1536]{1,0:T(8,128)(2,1)}, bf16[768,1536]{1,0:T(8,128)(2,1)}, u32[]{:S(2)}, u32[]{:S(2)}) collective-permute-start(bf16[768,1536]{1,0:T(8,128)(2,1)} %get-tuple-element.41), channel_id=1, source_target_pairs={{0,24},{8,0},{16,8},{24,16},{1,25},{9,1},{17,9},{25,17},{2,26},{10... | collective-permute-start | bytes 7077896 | tf_op jit(solution)/shard_map/ppermute | solution.py:410
  167.0 52.8 %collective-permute-start.9 = (bf16[2,6,128,256]{3,2,1,0:T(8,128)(2,1)}, bf16[2,6,128,256]{3,2,1,0:T(8,128)(2,1)S(1)}, u32[]{:S(2)}, u32[]{:S(2)}) collective-permute-start(bf16[2,6,128,256]{3,2,1,0:T(8,128)(2,1)} %collective-permute-done.4.refs_0_), channel_id=1, source_target_pairs={{0,1},{1,0},{2,3},{3,2},{4,5},{5,4},{6,7},{7,6},{8,9},{9,8},{10,11... | collective-permute-start | bytes 2359304 | tf_op jit(solution)/shard_map/ppermute | solution.py:387
  193.4 26.4 %copy-start.5 = (bf16[2,6,128,256]{3,2,1,0:T(8,128)(2,1)S(1)}, bf16[2,6,128,256]{3,2,1,0:T(8,128)(2,1)}, u32[]{:S(2)}) copy-start(bf16[2,6,128,256]{3,2,1,0:T(8,128)(2,1)} %copy-done.4) | copy-start | bytes 2359300
  219.8 0.9 copy-start.7
  219.8 27.2 %collective-permute-start.11 = (bf16[2,6,128,256]{3,2,1,0:T(8,128)(2,1)S(1)}, bf16[2,6,128,256]{3,2,1,0:T(8,128)(2,1)}, u32[]{:S(2)}, u32[]{:S(2)}) collective-permute-start(bf16[2,6,128,256]{3,2,1,0:T(8,128)(2,1)S(1)} %copy-done.5), channel_id=1, source_target_pairs={{0,1},{1,0},{2,3},{3,2},{4,5},{5,4},{6,7},{7,6},{8,9},{9,8},{10,11... | collective-permute-start | bytes 2359304 | tf_op jit(solution)/shard_map/ppermute | solution.py:387
  247.0 59.6 %collective-permute-start.3 = (f32[2,136,1536]{2,1,0:T(8,128)}, f32[2,136,1536]{2,1,0:T(8,128)}, u32[]{:S(2)}, u32[]{:S(2)}) collective-permute-start(f32[2,136,1536]{2,1,0:T(8,128)} %attend.10), channel_id=1, source_target_pairs={{0,4},{1,5},{2,6},{3,7},{4,0},{5,1},{6,2},{7,3},{8,12},{9,13},{10,... | collective-permute-start | bytes 5013512 | tf_op jit(solution)/shard_map/ppermute | solution.py:387
  302.4 4.2 collective-permute-start.17
  302.6 38.6 %collective-permute-start.12 = (f32[2,136,1536]{2,1,0:T(8,128)}, f32[2,136,1536]{2,1,0:T(8,128)}, u32[]{:S(2)}, u32[]{:S(2)}) collective-permute-start(f32[2,136,1536]{2,1,0:T(8,128)} %attend.14), channel_id=1, source_target_pairs={{0,3},{1,2},{2,5},{3,4},{4,7},{5,6},{6,1},{7,0},{8,11},{9,10},{10,... | collective-permute-start | bytes 5013512 | tf_op jit(solution)/shard_map/ppermute | solution.py:387
  303.3 39.7 %collective-permute-start.10 = (f32[2,136,1536]{2,1,0:T(8,128)}, f32[2,136,1536]{2,1,0:T(8,128)}, u32[]{:S(2)}, u32[]{:S(2)}) collective-permute-start(f32[2,136,1536]{2,1,0:T(8,128)} %attend.13), channel_id=1, source_target_pairs={{0,7},{1,6},{2,1},{3,0},{4,3},{5,2},{6,5},{7,4},{8,15},{9,14},{10,... | collective-permute-start | bytes 5013512 | tf_op jit(solution)/shard_map/ppermute | solution.py:387
  304.3 73.2 %collective-permute-start.8 = (f32[2,136,1536]{2,1,0:T(8,128)}, f32[2,136,1536]{2,1,0:T(8,128)}, u32[]{:S(2)}, u32[]{:S(2)}) collective-permute-start(f32[2,136,1536]{2,1,0:T(8,128)} %attend.12), channel_id=1, source_target_pairs={{0,2},{1,3},{2,4},{3,5},{4,6},{5,7},{6,0},{7,1},{8,10},{9,11},{10,... | collective-permute-start | bytes 5013512 | tf_op jit(solution)/shard_map/ppermute | solution.py:387
  306.6 112.1 %collective-permute-start.18 = (bf16[768,1536]{1,0:T(8,128)(2,1)}, bf16[768,1536]{1,0:T(8,128)(2,1)S(1)}, u32[]{:S(2)}, u32[]{:S(2)}) collective-permute-start(bf16[768,1536]{1,0:T(8,128)(2,1)} %collective-permute-done.14.refs_10_), channel_id=1, source_target_pairs={{0,1},{1,0},{2,3},{3,2},{4,5},{5,4},{6,7},{7,6},{8,9},{9,8},{10,11... | collective-permute-start | bytes 7077896 | tf_op jit(solution)/shard_map/ppermute | solution.py:421
  306.6 112.1 %collective-permute-start.19 = (bf16[768,1536]{1,0:T(8,128)(2,1)}, bf16[768,1536]{1,0:T(8,128)(2,1)}, u32[]{:S(2)}, u32[]{:S(2)}) collective-permute-start(bf16[768,1536]{1,0:T(8,128)(2,1)} %collective-permute-done.15.refs_11_), channel_id=1, source_target_pairs={{0,1},{1,0},{2,3},{3,2},{4,5},{5,4},{6,7},{7,6},{8,9},{9,8},{10,11... | collective-permute-start | bytes 7077896 | tf_op jit(solution)/shard_map/ppermute | solution.py:421
  341.2 77.5 %collective-permute-start.20 = (bf16[768,1536]{1,0:T(8,128)(2,1)}, bf16[768,1536]{1,0:T(8,128)(2,1)}, u32[]{:S(2)}, u32[]{:S(2)}) collective-permute-start(bf16[768,1536]{1,0:T(8,128)(2,1)} %collective-permute-done.16.refs_12_), channel_id=1, source_target_pairs={{0,1},{1,0},{2,3},{3,2},{4,5},{5,4},{6,7},{7,6},{8,9},{9,8},{10,11... | collective-permute-start | bytes 7077896 | tf_op jit(solution)/shard_map/ppermute | solution.py:421
  342.9 40.9 %collective-permute-start.7 = (f32[2,136,1536]{2,1,0:T(8,128)}, f32[2,136,1536]{2,1,0:T(8,128)}, u32[]{:S(2)}, u32[]{:S(2)}) collective-permute-start(f32[2,136,1536]{2,1,0:T(8,128)} %attend.11), channel_id=1, source_target_pairs={{0,6},{1,7},{2,0},{3,1},{4,2},{5,3},{6,4},{7,5},{8,14},{9,15},{10,... | collective-permute-start | bytes 5013512 | tf_op jit(solution)/shard_map/ppermute | solution.py:387
  377.5 41.2 %collective-permute-start.6 = (f32[2,136,1536]{2,1,0:T(8,128)}, f32[2,136,1536]{2,1,0:T(8,128)}, u32[]{:S(2)}, u32[]{:S(2)}) collective-permute-start(f32[2,136,1536]{2,1,0:T(8,128)} %collective-permute-done.5), channel_id=1, source_target_pairs={{0,7},{1,6},{2,1},{3,0},{4,3},{5,2},{6,5},{7,4},{8,15},{9,14},{10,... | collective-permute-start | bytes 5013512 | tf_op jit(solution)/shard_map/ppermute | solution.py:387
  418.7 1.4 copy-start.3
  420.1 68.0 %copy-start.1 = (f32[256,64]{0,1:T(8,128)S(1)}, f32[256,64]{0,1:T(8,128)}, u32[]{:S(2)}) copy-start(f32[256,64]{0,1:T(8,128)} %param.11) | copy-start | bytes 196612
